TPU v7x, 32 devices: a whole 2x2x4 slice. The times are simulated.
32 devices in a mesh: dp: 16 (over z, y, core), tensor: 2 (over x).
Axes of the slice: x: 2, y: 2, z: 4, core: 2. Of those that a mesh axis runs over, the one named last changes fastest.
Arguments:
- tokens: float32 [2, 25600, 512], P(None, ('dp', 'tensor')), may hold values from -6 to 6
- key_mask: int32 [2, 128, 200], P(None, 'dp'), may hold values from 0 to 1, as said below
- expert_ids: int32 [2, 25600, 2], P(None, 'dp'), may hold values from 0 to 31, as said below
- slot_ids: int32 [2, 25600, 2], P(None, 'dp'), may hold values from -1 to 119, as said below
- norm1_gain: float32 [512], P(('dp', 'tensor')), may hold values from 0.25 to 1.75
- norm1_bias: float32 [512], P(('dp', 'tensor')), may hold values from -3 to 3
- qkv_weight: bfloat16 [512, 3, 512], P('dp', None, 'tensor'), may hold values from -0.25 to 0.25
- out_weight: bfloat16 [512, 512], P('tensor', 'dp'), may hold values from -1 to 1
- norm2_gain: float32 [512], P(('dp', 'tensor')), may hold values from 0.25 to 1.75
- norm2_bias: float32 [512], P(('dp', 'tensor')), may hold values from -3 to 3
- router_weight: float32 [512, 32], P(('dp', 'tensor')), may hold values from -0.25 to 0.25
- expert_in: bfloat16 [32, 512, 2048], P(None, 'dp', 'tensor'), may hold values from -0.25 to 0.25
- expert_out: bfloat16 [32, 2048, 512], P(None, 'tensor', 'dp'), may hold values from -3 to 3
- cotangent: float32 [2, 25600, 512], P(None, ('dp', 'tensor')), may hold values from -6 to 6
Outputs:
- block_out: float32 [2, 25600, 512], P(None, ('dp', 'tensor'))
- input_grad: float32 [2, 25600, 512], P(None, ('dp', 'tensor'))
- norm1_gain_grad: float32 [512], P(('dp', 'tensor'))
- norm1_bias_grad: float32 [512], P(('dp', 'tensor'))
- qkv_grad: float32 [512, 3, 512], P('dp', None, 'tensor')
- out_grad: float32 [512, 512], P('tensor', 'dp')
- norm2_gain_grad: float32 [512], P(('dp', 'tensor'))
- norm2_bias_grad: float32 [512], P(('dp', 'tensor'))
- router_grad: float32 [512, 32], P(('dp', 'tensor'))
- expert_in_grad: float32 [32, 512, 2048], P(None, 'dp', 'tensor')
- expert_out_grad: float32 [32, 2048, 512], P(None, 'tensor', 'dp')
Inputs may be any that keep to these rules, and one draw needn't show every extreme that they name: `key_mask`: position 0 of every image is 1; positions 197 to 199 are 0. `expert_ids`: each row names two different experts. `slot_ids`: slots count within routing groups of 1600 consecutive rows of a micro-batch. -1 marks a dropped route; no two other routes of a group share expert and slot, and the slots used by one expert in a group are 0, 1, 2, ... without gaps.
All inputs are finite; a program needn't handle non-finite values.
Results may differ from a plain program's by a relative error of at most 0.035.
Values may be sent and summed in bfloat16 or wider, within the bound.
A program may use at most 264 MiB of HBM per device.

v0:
```python
import jax
import jax.numpy as jnp
from jax import lax
from jax.sharding import PartitionSpec as P

HEAD = 64
CAP = 120
EPSILON = 1e-06
FIRST_DIMS = (((0,), (0,)), ((), ()))
LAST_DIMS = (((1,), (1,)), ((), ()))


def norm_rows(values, gain, offset):
    center = jnp.mean(values, -1, keepdims=True)
    shifted = values - center
    spread = jnp.mean(shifted * shifted, -1, keepdims=True)
    return shifted * lax.rsqrt(spread + EPSILON) * gain + offset


def slot_table(routes, slot_count):
    places = lax.broadcasted_iota(jnp.int32, (routes.shape[0], slot_count), 1)
    hits = (routes[:, 0:1] == places) | (routes[:, 1:2] == places)
    return hits.astype(jnp.bfloat16)


def per_device(
    tokens,
    key_mask,
    expert_ids,
    slot_ids,
    norm1_gain,
    norm1_bias,
    qkv_weight,
    out_weight,
    norm2_gain,
    norm2_bias,
    router_weight,
    expert_in,
    expert_out,
    cotangent,
):
    highest = lax.Precision.HIGHEST
    gain_one, bias_one, gain_two, bias_two, router_full = (
        lax.all_gather(norm1_gain, ("dp", "tensor"), axis=0, tiled=True),
        lax.all_gather(norm1_bias, ("dp", "tensor"), axis=0, tiled=True),
        lax.all_gather(norm2_gain, ("dp", "tensor"), axis=0, tiled=True),
        lax.all_gather(norm2_bias, ("dp", "tensor"), axis=0, tiled=True),
        lax.all_gather(router_weight, ("dp", "tensor"), axis=0, tiled=True),
    )
    micro_count, own_rows, model_width = tokens.shape
    image_count, seq_length = (key_mask.shape[1], key_mask.shape[2])
    group_rows = image_count * seq_length
    expert_count = expert_in.shape[0]
    hidden_width = expert_in.shape[2]
    slot_count = expert_count * CAP
    head_width = qkv_weight.shape[2]
    local_heads = head_width // HEAD
    scaling = HEAD ** (-0.5)
    own_start = lax.axis_index("tensor") * own_rows

    def fetch_attention():
        qkv_full, attn_full = (
            lax.all_gather(qkv_weight, "dp", axis=0, tiled=True),
            lax.all_gather(out_weight, "dp", axis=1, tiled=True),
        )
        qkv_every, attn_every = (None, None)
        return (qkv_full.reshape(model_width, 3 * head_width), attn_full, qkv_every, attn_every)

    def current_weights():
        return (
            fetch_attention(),
            (
                lax.all_gather(expert_in, "dp", axis=1, tiled=True),
                lax.all_gather(expert_out, "dp", axis=2, tiled=True),
            ),
        )

    qkv_acc = jnp.zeros((model_width, 3 * head_width), jnp.float32)
    attn_acc = jnp.zeros((head_width, model_width), jnp.float32)
    first_acc = jnp.zeros((expert_count, model_width, hidden_width), jnp.float32)
    second_acc = jnp.zeros((expert_count, hidden_width, model_width), jnp.float32)
    router_acc = jnp.zeros((model_width, expert_count), jnp.float32)
    gain_one_acc = jnp.zeros((model_width,), jnp.float32)
    bias_one_acc = jnp.zeros((model_width,), jnp.float32)
    gain_two_acc = jnp.zeros((model_width,), jnp.float32)
    bias_two_acc = jnp.zeros((model_width,), jnp.float32)
    block_list = []
    grad_list = []
    for micro_step in range(micro_count):
        row_block = tokens[micro_step]
        cot_block = cotangent[micro_step]
        key_flags = key_mask[micro_step]
        experts = expert_ids[micro_step]
        places = slot_ids[micro_step]
        retained = (places >= 0).astype(jnp.float32)
        slot_index = jnp.where(places >= 0, experts * CAP + places, slot_count)

        def masked_scores(query, keyed):
            raw = (
                jnp.einsum("bqhd,bkhd->bhqk", query, keyed, preferred_element_type=jnp.float32)
                * scaling
            )
            return jnp.where(key_flags[:, None, None, :] > 0, raw, -1e30)

        (qkv_joined, attn_local, qkv_every, attn_every), (first_layer, second_layer) = (
            current_weights()
        )
        normed_own = norm_rows(row_block, gain_one, bias_one).astype(jnp.bfloat16)
        normed_all = lax.all_gather(normed_own, "tensor", axis=0, tiled=True)
        projected = jnp.dot(normed_all, qkv_joined, preferred_element_type=jnp.float32).astype(
            jnp.bfloat16
        )
        projected = projected.reshape(image_count, seq_length, 3, local_heads, HEAD)
        query, keyed, valued = (projected[:, :, 0], projected[:, :, 1], projected[:, :, 2])
        scores = masked_scores(query, keyed)
        row_max = jnp.max(scores, -1, keepdims=True)
        lifted = jnp.exp(scores - row_max)
        row_total = jnp.sum(lifted, -1, keepdims=True)
        probs = lifted / row_total
        log_total = row_max + jnp.log(row_total)
        mixed = jnp.einsum(
            "bhqk,bkhd->bqhd",
            probs.astype(jnp.bfloat16),
            valued,
            preferred_element_type=jnp.float32,
        )
        mixed = mixed.astype(jnp.bfloat16).reshape(group_rows, head_width)
        middle = row_block + lax.psum_scatter(
            jnp.dot(mixed, attn_local, preferred_element_type=jnp.float32).astype(jnp.bfloat16),
            "tensor",
            scatter_dimension=0,
            tiled=True,
        ).astype(jnp.float32)
        routed_own = norm_rows(middle, gain_two, bias_two).astype(jnp.bfloat16)
        piece = lax.all_gather(routed_own, "tensor", axis=0, tiled=True)
        count = piece.shape[0]
        gates = jax.nn.softmax(
            jnp.dot(piece.astype(jnp.float32), router_full, precision=highest), axis=-1
        )
        picks = lax.broadcasted_iota(jnp.int32, (count, 2, expert_count), 2) == experts[:, :, None]
        picked_gates = jnp.sum(jnp.where(picks, gates[:, None, :], 0.0), -1) * retained
        chosen = picked_gates
        table = slot_table(slot_index, slot_count)
        dispatched = lax.dot_general(table, piece, FIRST_DIMS, preferred_element_type=jnp.float32)
        dispatched, chosen = (dispatched, chosen)
        slot_gate = (
            jnp.zeros((slot_count + 1,), jnp.float32)
            .at[slot_index.reshape(-1)]
            .set(chosen.reshape(-1))[:slot_count]
        )
        dispatched_low = dispatched.astype(jnp.bfloat16).reshape(expert_count, CAP, model_width)
        hidden_pre = jnp.einsum(
            "ecd,edf->ecf", dispatched_low, first_layer, preferred_element_type=jnp.float32
        )
        hidden = jax.nn.gelu(hidden_pre).astype(jnp.bfloat16)
        expert_part = jnp.einsum(
            "ecf,efd->ecd", hidden, second_layer, preferred_element_type=jnp.float32
        ).reshape(slot_count, model_width)
        weighted = jnp.concatenate(
            [slot_gate[:, None] * expert_part, jnp.zeros((1, model_width), jnp.float32)], 0
        )
        block_list.append(
            middle
            + lax.psum_scatter(
                (weighted[slot_index[:, 0]] + weighted[slot_index[:, 1]]).astype(jnp.bfloat16),
                "tensor",
                scatter_dimension=0,
                tiled=True,
            ).astype(jnp.float32)
        )
        (qkv_joined, attn_local, qkv_every, attn_every), (first_layer, second_layer) = (
            current_weights()
        )
        cot_low = cot_block.astype(jnp.bfloat16)
        picked_grads = lax.dot_general(
            slot_table(slot_index, slot_count),
            lax.all_gather(cot_low, "tensor", axis=0, tiled=True),
            FIRST_DIMS,
            preferred_element_type=jnp.float32,
        )
        gate_part = jnp.sum(picked_grads * expert_part, -1)
        result_grad = (
            (slot_gate[:, None] * picked_grads)
            .astype(jnp.bfloat16)
            .reshape(expert_count, CAP, model_width)
        )
        hidden_grad = jnp.einsum(
            "ecd,efd->ecf", result_grad, second_layer, preferred_element_type=jnp.float32
        )
        pre_grad = jax.vjp(jax.nn.gelu, hidden_pre)[1](hidden_grad)[0].astype(jnp.bfloat16)
        first_acc = first_acc + jnp.einsum(
            "ecd,ecf->edf", dispatched_low, pre_grad, preferred_element_type=jnp.float32
        )
        second_acc = second_acc + jnp.einsum(
            "ecf,ecd->efd", hidden, result_grad, preferred_element_type=jnp.float32
        )
        dispatch_grad = jnp.einsum(
            "ecf,edf->ecd", pre_grad, first_layer, preferred_element_type=jnp.float32
        ).reshape(slot_count, model_width)
        dispatch_grad = jnp.concatenate(
            [dispatch_grad, jnp.zeros((1, model_width), jnp.float32)], 0
        )
        gate_padded = jnp.concatenate([gate_part, jnp.zeros((1,), jnp.float32)], 0)
        row_grads = dispatch_grad[slot_index[:, 0]] + dispatch_grad[slot_index[:, 1]]
        gate_grads = gate_padded[slot_index]
        own_row_grads, own_gate_grads = (
            lax.psum_scatter(
                row_grads.astype(jnp.bfloat16), "tensor", scatter_dimension=0, tiled=True
            ).astype(jnp.float32),
            lax.psum_scatter(
                gate_grads.astype(jnp.bfloat16), "tensor", scatter_dimension=0, tiled=True
            ).astype(jnp.float32),
        )
        own_experts = lax.dynamic_slice_in_dim(experts, own_start, own_rows, 0)
        routed_wide = routed_own.astype(jnp.float32)
        own_gates = jax.nn.softmax(jnp.dot(routed_wide, router_full, precision=highest), axis=-1)
        own_picks = (
            lax.broadcasted_iota(jnp.int32, (own_rows, 2, expert_count), 2)
            == own_experts[:, :, None]
        )
        gate_cot = jnp.sum(jnp.where(own_picks, own_gate_grads[:, :, None], 0.0), 1)
        logit_grad = own_gates * (gate_cot - jnp.sum(own_gates * gate_cot, -1, keepdims=True))
        routed_grad = own_row_grads + jnp.dot(logit_grad, router_full.T, precision=highest)
        router_acc = router_acc + jnp.dot(routed_wide.T, logit_grad, precision=highest)
        middle_part, gain_step, bias_step = jax.vjp(norm_rows, middle, gain_two, bias_two)[1](
            routed_grad
        )
        gain_two_acc = gain_two_acc + gain_step
        bias_two_acc = bias_two_acc + bias_step
        middle_grad = cot_block + middle_part
        attn_cot = lax.all_gather(middle_grad.astype(jnp.bfloat16), "tensor", axis=0, tiled=True)
        attn_acc = attn_acc + lax.dot_general(
            mixed, attn_cot, FIRST_DIMS, preferred_element_type=jnp.float32
        )
        mixed_grad = lax.dot_general(
            attn_cot, attn_local, LAST_DIMS, preferred_element_type=jnp.float32
        )
        mixed_grad = mixed_grad.astype(jnp.bfloat16).reshape(
            image_count, seq_length, local_heads, HEAD
        )
        again_probs = jnp.exp(masked_scores(query, keyed) - log_total)
        prob_grad = jnp.einsum(
            "bqhd,bkhd->bhqk", mixed_grad, valued, preferred_element_type=jnp.float32
        )
        value_grad = jnp.einsum(
            "bhqk,bqhd->bkhd",
            again_probs.astype(jnp.bfloat16),
            mixed_grad,
            preferred_element_type=jnp.float32,
        ).astype(jnp.bfloat16)
        inner_sum = jnp.sum(again_probs * prob_grad, -1, keepdims=True)
        score_grad = (again_probs * (prob_grad - inner_sum)).astype(jnp.bfloat16)
        query_grad = (
            jnp.einsum("bhqk,bkhd->bqhd", score_grad, keyed, preferred_element_type=jnp.float32)
            * scaling
        ).astype(jnp.bfloat16)
        keyed_grad = (
            jnp.einsum("bhqk,bqhd->bkhd", score_grad, query, preferred_element_type=jnp.float32)
            * scaling
        ).astype(jnp.bfloat16)
        proj_grad = jnp.stack([query_grad, keyed_grad, value_grad], 2).reshape(
            group_rows, 3 * head_width
        )
        qkv_acc = qkv_acc + lax.dot_general(
            normed_all, proj_grad, FIRST_DIMS, preferred_element_type=jnp.float32
        )
        normed_grad = lax.psum_scatter(
            lax.dot_general(
                proj_grad, qkv_joined, LAST_DIMS, preferred_element_type=jnp.float32
            ).astype(jnp.bfloat16),
            "tensor",
            scatter_dimension=0,
            tiled=True,
        ).astype(jnp.float32)
        input_part, gain_step, bias_step = jax.vjp(norm_rows, row_block, gain_one, bias_one)[1](
            normed_grad
        )
        gain_one_acc = gain_one_acc + gain_step
        bias_one_acc = bias_one_acc + bias_step
        grad_list.append(middle_grad + input_part)
    qkv_grad, out_grad, first_grad, second_grad = (
        lax.psum_scatter(
            qkv_acc.reshape(model_width, 3, head_width).astype(jnp.bfloat16),
            "dp",
            scatter_dimension=0,
            tiled=True,
        ).astype(jnp.float32),
        lax.psum_scatter(
            attn_acc.astype(jnp.bfloat16), "dp", scatter_dimension=1, tiled=True
        ).astype(jnp.float32),
        lax.psum_scatter(
            first_acc.astype(jnp.bfloat16), "dp", scatter_dimension=1, tiled=True
        ).astype(jnp.float32),
        lax.psum_scatter(
            second_acc.astype(jnp.bfloat16), "dp", scatter_dimension=2, tiled=True
        ).astype(jnp.float32),
    )
    gain_one_grad, bias_one_grad, gain_two_grad, bias_two_grad, router_grad = (
        lax.psum_scatter(gain_one_acc, ("dp", "tensor"), scatter_dimension=0, tiled=True),
        lax.psum_scatter(bias_one_acc, ("dp", "tensor"), scatter_dimension=0, tiled=True),
        lax.psum_scatter(gain_two_acc, ("dp", "tensor"), scatter_dimension=0, tiled=True),
        lax.psum_scatter(bias_two_acc, ("dp", "tensor"), scatter_dimension=0, tiled=True),
        lax.psum_scatter(router_acc, ("dp", "tensor"), scatter_dimension=0, tiled=True),
    )
    return (
        jnp.stack(block_list),
        jnp.stack(grad_list),
        gain_one_grad,
        bias_one_grad,
        qkv_grad,
        out_grad,
        gain_two_grad,
        bias_two_grad,
        router_grad,
        first_grad,
        second_grad,
    )


def solution(mesh):
    placed = (
        P(None, ("dp", "tensor"), None),
        P(None, "dp", None),
        P(None, "dp", None),
        P(None, "dp", None),
        P(("dp", "tensor")),
        P(("dp", "tensor")),
        P("dp", None, "tensor"),
        P("tensor", "dp"),
        P(("dp", "tensor")),
        P(("dp", "tensor")),
        P(("dp", "tensor"), None),
        P(None, "dp", "tensor"),
        P(None, "tensor", "dp"),
        P(None, ("dp", "tensor"), None),
    )
    return jax.shard_map(
        per_device,
        mesh=mesh,
        in_specs=placed,
        out_specs=(
            P(None, ("dp", "tensor"), None),
            P(None, ("dp", "tensor"), None),
            P(("dp", "tensor")),
            P(("dp", "tensor")),
            P("dp", None, "tensor"),
            P("tensor", "dp"),
            P(("dp", "tensor")),
            P(("dp", "tensor")),
            P(("dp", "tensor"), None),
            P(None, "dp", "tensor"),
            P(None, "tensor", "dp"),
        ),
        check_vma=False,
    )
```

profile of v0, /device:TPU:0, one launch (start us, length us, event | category | flops | bytes accessed | tf_op | source)
XLA Modules:
  0.0 2154.3 jit_solution(1419710168144649038)
XLA Ops:
  12.3 42.0 %all-reduce.14 = (f32[512]{0:T(512)S(1)}, f32[512]{0:T(512)S(1)}, f32[512]{0:T(512)S(1)}, f32[512]{0:T(512)S(1)}) all-reduce(f32[512]{0:T(512)S(1)} %dynamic-update-slice.1, f32[512]{0:T(512)S(1)} %dynamic-update-slice, f32[512]{0:T(512)S(1)} %dynamic-update-slice.3, ...), channel_id=1, replica_groups=mesh['dp'=16,'tensor'=2] {'dp','tensor'}, use_global_device_ids=true, to_apply=%add.5 | all-reduce | flops 2048 | bytes 16384
  56.8 22.0 %all_gather.67 = bf16[256,512]{0,1:T(8,128)(2,1)S(1)} all-gather(bf16[256,32]{0,1:T(8,128)(2,1)} %param.21), channel_id=1, replica_groups=mesh['dp'=16,'tensor'=2] {'dp'}, dimensions={1}, use_global_device_ids=true | all-gather | bytes 278528 | tf_op jit(solution)/shard_map/all_gather | solution.py:64
  78.8 21.7 %all_gather.66 = bf16[512,3,256]{2,0,1:T(8,128)(2,1)} all-gather(bf16[32,3,256]{2,0,1:T(8,128)(2,1)} %param.20), channel_id=1, replica_groups=mesh['dp'=16,'tensor'=2] {'dp'}, dimensions={0}, use_global_device_ids=true | all-gather | bytes 835584 | tf_op jit(solution)/shard_map/all_gather | solution.py:63
  107.4 8.2 reshape.604
  151.3 8.2 reshape.605
  190.5 24.6 %reduce-scatter.23.cloned.1.call-done = bf16[800,512]{1,0:T(8,128)(2,1)} async-done(((bf16[1600,512]{1,0:T(8,128)(2,1)}), bf16[800,512]{1,0:T(8,128)(2,1)}) %reduce-scatter.23.cloned.1.call-update) | async-done | bytes 819216 | tf_op jit(solution)/shard_map/reduce_scatter | solution.py:128
  228.6 69.3 %all_gather.71 = f32[512,32]{1,0:T(8,128)S(1)} all-gather(f32[16,32]{1,0:T(8,128)S(1)} %copy-done.106), channel_id=1, replica_groups=mesh['dp'=16,'tensor'=2] {'dp','tensor'}, dimensions={0}, use_global_device_ids=true | all-gather | bytes 67584 | tf_op jit(solution)/shard_map/all_gather | solution.py:48
  310.7 16.4 scatter_custom_fusion
  327.1 16.2 scatter_custom_fusion.1
  343.4 10.5 fusion.34
  353.8 10.7 fusion.37
  364.6 87.7 %all-gather.15.cloned.1.call-done = bf16[32,512,1024]{2,1,0:T(8,128)(2,1)} async-done(((bf16[32,32,1024]{2,1,0:T(8,128)(2,1)}), bf16[32,512,1024]{2,1,0:T(8,128)(2,1)}) %all-gather.15.cloned.1.call-update) | async-done | bytes 33554448 | tf_op jit(solution)/shard_map/all_gather | solution.py:73
  452.2 21.3 fusion.145
  473.5 148.3 %all-gather.17.cloned.1.call-done = bf16[32,1024,512]{1,2,0:T(8,128)(2,1)} async-done(((bf16[32,1024,32]{1,2,0:T(8,128)(2,1)}), bf16[32,1024,512]{1,2,0:T(8,128)(2,1)}) %all-gather.17.cloned.1.call-update) | async-done | bytes 33554448 | tf_op jit(solution)/shard_map/all_gather | solution.py:74
  621.8 23.1 %fusion.130 = f32[32,120,512]{2,1,0:T(8,128)} fusion(bf16[32,1024,512]{1,2,0:T(8,128)(2,1)} %all-gather.17.cloned.1.call-done, f32[32,120,1024]{2,1,0:T(8,128)} %fusion.145), kind=kOutput, calls=%fused_computation.282 | convolution fusion | flops 4061921280 | bytes 57147392 | tf_op jit(solution)/shard_map/ecf,efd->ecd/dot_general | solution.py:156
  651.9 17.7 fusion.32
  669.6 19.2 gather_fusion.9
  690.5 20.8 fusion.144
  711.3 22.2 %fusion.129 = f32[32,120,512]{2,1,0:T(8,128)} fusion(bf16[32,1024,512]{1,2,0:T(8,128)(2,1)} %all-gather.17.cloned.1.call-done, f32[32,120,1024]{2,1,0:T(8,128)} %fusion.144), kind=kOutput, calls=%fused_computation.281 | convolution fusion | flops 4061921280 | bytes 57147392 | tf_op jit(solution)/shard_map/ecf,efd->ecd/dot_general | solution.py:156
  733.6 16.6 fusion.33
  752.0 24.5 %fusion.16 = bf16[32,120,1024]{2,1,0:T(8,128)(2,1)} fusion(f32[32,120,1024]{2,1,0:T(8,128)} %fusion.144, bf16[32,120,512]{2,1,0:T(8,128)(2,1)S(1)} %bitcast.286, bf16[32,1024,512]{1,2,0:T(8,128)(2,1)} %all-gather.17.cloned.1.call-done), kind=kOutput, calls=%fused_computation.34 | convolution fusion | flops 4105175040 | bytes 61079552 | tf_op jit(solution)/shard_map/ecd,efd->ecf/dot_general | solution.py:187
  776.6 21.0 fusion.146
  797.6 19.2 gather_fusion.6
  818.4 7.3 concatenate.20
  825.7 9.0 gather_fusion.5
  834.8 9.6 gather_fusion.4
  848.1 24.2 %fusion.23 = bf16[32,120,1024]{2,1,0:T(8,128)(2,1)} fusion(f32[32,120,1024]{2,1,0:T(8,128)} %fusion.145, bf16[32,120,512]{2,1,0:T(8,128)(2,1)} %bitcast.288, bf16[32,1024,512]{1,2,0:T(8,128)(2,1)} %all-gather.17.cloned.1.call-done), kind=kOutput, calls=%fused_computation.41 | convolution fusion | flops 4105175040 | bytes 61079552 | tf_op jit(solution)/shard_map/ecd,efd->ecf/dot_general | solution.py:187
  872.3 21.0 fusion.147
  893.4 7.3 concatenate.22
  900.7 9.0 gather_fusion.8
  909.7 9.6 gather_fusion.7
  930.4 9.4 gather_fusion.3
  939.8 9.6 gather_fusion.2
  960.5 9.0 gather_fusion.1
  969.6 9.6 gather_fusion
  1020.4 27.1 %all-gather.25.cloned.1.call-done = bf16[1600,512]{1,0:T(8,128)(2,1)} async-done(((bf16[800,512]{1,0:T(8,128)(2,1)}), bf16[1600,512]{1,0:T(8,128)(2,1)}) %all-gather.25.cloned.1.call-update) | async-done | bytes 1638416 | tf_op jit(solution)/shard_map/all_gather | solution.py:231
  1051.2 7.5 multiply_reduce_fusion.1
  1069.3 8.0 all-gather.29.cloned.1.call-done
  1139.9 30.2 %fusion.128 = f32[32,1024,512]{1,2,0:T(8,128)} fusion(bf16[32,120,512]{2,1,0:T(8,128)(2,1)} %bitcast.287, f32[32,120,1024]{2,1,0:T(8,128)} %fusion.144), kind=kOutput, calls=%fused_computation.280 | convolution fusion | flops 4061921280 | bytes 86769664 | tf_op jit(solution)/shard_map/ecf,ecd->efd/dot_general | solution.py:194
  1172.9 40.5 %add_convert_fusion = bf16[32,1024,512]{1,2,0:T(8,128)(2,1)} fusion(f32[32,1024,512]{1,2,0:T(8,128)} %fusion.128, bf16[32,120,512]{2,1,0:T(8,128)(2,1)} %bitcast.289, f32[32,120,1024]{2,1,0:T(8,128)} %fusion.145), kind=kOutput, calls=%fused_computation.12 | convolution fusion | flops 4095475712 | bytes 120324096 | tf_op jit(solution)/shard_map/ecf,ecd->efd/dot_general | solution.py:194
  1213.4 27.6 %fusion.150 = f32[32,512,1024]{2,1,0:T(8,128)} fusion(bf16[32,120,512]{2,1,0:T(8,128)(2,1)} %bitcast.285, bf16[32,120,1024]{2,1,0:T(8,128)(2,1)} %fusion.16), kind=kOutput, calls=%fused_computation.302 | convolution fusion | flops 4026531840 | bytes 78905344 | tf_op jit(solution)/shard_map/ecd,ecf->edf/dot_general | solution.py:191
  1241.1 37.5 %add_convert_fusion.1 = bf16[32,512,1024]{2,1,0:T(8,128)(2,1)} fusion(f32[32,512,1024]{2,1,0:T(8,128)} %fusion.150, bf16[32,120,512]{2,1,0:T(8,128)(2,1)} %bitcast.283, bf16[32,120,1024]{2,1,0:T(8,128)(2,1)} %fusion.23), kind=kOutput, calls=%fused_computation.13 | convolution fusion | flops 4060086272 | bytes 112459776 | tf_op jit(solution)/shard_map/ecd,ecf->edf/dot_general | solution.py:191
  1290.6 21.1 reduce-scatter.29.cloned.1.call-done
  1311.7 29.7 %reduce-scatter.33.cloned.1.call-done = bf16[800,512]{1,0:T(8,128)(2,1)} async-done(((bf16[1600,512]{1,0:T(8,128)(2,1)}), bf16[800,512]{1,0:T(8,128)(2,1)}) %reduce-scatter.33.cloned.1.call-update) | async-done | bytes 819216 | tf_op jit(solution)/shard_map/reduce_scatter | solution.py:267
  1345.8 39.4 %all-reduce.13 = (f32[512]{0:T(512)S(1)}, f32[512]{0:T(512)S(1)}, f32[512]{0:T(512)S(1)}, f32[512]{0:T(512)S(1)}) all-reduce(f32[512]{0:T(512)S(1)} %add.372, f32[512]{0:T(512)S(1)} %add.373, f32[512]{0:T(512)S(1)} %add.376, f32[512]{0:T(512)S(1)} %add.377), channel_id=12, replica_groups=mesh['dp'=16,'tensor'=2] {'dp','tensor'}, use_global_device_ids=true, to_apply=%region_52.53.clone | all-reduce | flops 2048 | bytes 16384
  1395.1 281.1 %reduce-scatter.41.cloned.1.call-done = bf16[32,1024,32]{1,2,0:T(8,128)(2,1)} async-done(((bf16[32,1024,512]{1,2,0:T(8,128)(2,1)}), bf16[32,1024,32]{1,2,0:T(8,128)(2,1)}) %reduce-scatter.41.cloned.1.call-update) | async-done | bytes 2097168 | tf_op jit(solution)/shard_map/reduce_scatter | solution.py:294
  1680.4 329.7 %reduce-scatter.39.cloned.1.call-done = bf16[32,32,1024]{2,1,0:T(8,128)(2,1)} async-done(((bf16[32,512,1024]{2,1,0:T(8,128)(2,1)}), bf16[32,32,1024]{2,1,0:T(8,128)(2,1)}) %reduce-scatter.39.cloned.1.call-update) | async-done | bytes 2097168 | tf_op jit(solution)/shard_map/reduce_scatter | solution.py:291
  2014.1 133.5 %reduce-scatter.37.cloned.1.call-done = f32[16,32]{1,0:T(8,128)} async-done(((f32[512,32]{1,0:T(8,128)}), f32[16,32]{1,0:T(8,128)}) %reduce-scatter.37.cloned.1.call-update) | async-done | bytes 2064 | tf_op jit(solution)/shard_map/reduce_scatter | solution.py:303
  (481 shorter events, 298.5 us)
Async XLA Ops:
  7.2 95.6 %all-gather.11.cloned.1.call-start = ((), (), s32[]{:S(2)}) async-start(), calls=%async_computation.14 | async-start | bytes 2457600 | tf_op jit(solution)/shard_map/all_gather | solution.py:109
  9.7 46.2 %copy-start.53 = (f32[800]{0:T(1024)}, f32[800]{0:T(1024)S(1)}, u32[]{:S(2)}) copy-start(f32[800]{0:T(1024)S(1)} %get-tuple-element.176) | copy-start | bytes 9604
  9.7 46.2 %copy-start.55 = (f32[800]{0:T(1024)}, f32[800]{0:T(1024)S(1)}, u32[]{:S(2)}) copy-start(f32[800]{0:T(1024)S(1)} %get-tuple-element.177) | copy-start | bytes 9604
  11.3 45.4 %copy-start.76 = (f32[800]{0:T(1024)}, f32[800]{0:T(1024)S(1)}, u32[]{:S(2)}) copy-start(f32[800]{0:T(1024)S(1)} %fusion.118) | copy-start | bytes 9604
  11.3 45.4 %copy-start.78 = (f32[800]{0:T(1024)}, f32[800]{0:T(1024)S(1)}, u32[]{:S(2)}) copy-start(f32[800]{0:T(1024)S(1)} %fusion.120) | copy-start | bytes 9604
  54.3 165.0 %copy-start.99 = (f32[512]{0:T(512)}, f32[512]{0:T(512)S(1)}, u32[]{:S(2)}) copy-start(f32[512]{0:T(512)S(1)} %get-tuple-element.101) | copy-start | bytes 6148
  56.0 90.8 %all-gather.19.cloned.1.call-start = ((), (), s32[]{:S(2)}) async-start(), calls=%async_computation.20 | async-start | bytes 2457600 | tf_op jit(solution)/shard_map/all_gather | solution.py:109
  56.7 133.8 %reduce-scatter.19.cloned.1.call-start = ((), (), s32[]{:S(2)}) async-start(), calls=%async_computation.15 | async-start | bytes 2457600 | tf_op jit(solution)/shard_map/reduce_scatter | solution.py:128
  78.8 108.7 %copy-start.27 = (bf16[256,512]{0,1:T(8,128)(2,1)}, bf16[256,512]{0,1:T(8,128)(2,1)S(1)}, u32[]{:S(2)}) copy-start(bf16[256,512]{0,1:T(8,128)(2,1)S(1)} %all_gather.67) | copy-start | bytes 786436
  146.5 68.6 %reduce-scatter.23.cloned.1.call-start = ((), (), s32[]{:S(2)}) async-start(), calls=%async_computation.21 | async-start | bytes 2457600 | tf_op jit(solution)/shard_map/reduce_scatter | solution.py:128
  190.5 112.4 %all-gather.21.cloned.1.call-start = ((), (), s32[]{:S(2)}) async-start(), calls=%async_computation.22 | async-start | bytes 2457600 | tf_op jit(solution)/shard_map/all_gather | solution.py:135
  221.6 84.3 %all-gather.13.cloned.1.call-start = ((), (), s32[]{:S(2)}) async-start(), calls=%async_computation.16 | async-start | bytes 2457600 | tf_op jit(solution)/shard_map/all_gather | solution.py:135
  222.1 230.1 %all-gather.15.cloned.1.call-start = ((), (), s32[]{:S(2)}) async-start(), calls=%async_computation.17 | async-start | bytes 35651584 | tf_op jit(solution)/shard_map/all_gather | solution.py:73
  222.9 398.9 %all-gather.17.cloned.1.call-start = ((), (), s32[]{:S(2)}) async-start(), calls=%async_computation.18 | async-start | bytes 35651584 | tf_op jit(solution)/shard_map/all_gather | solution.py:74
  223.7 428.2 %all-gather.27.cloned.1.call-start = ((), (), s32[]{:S(2)}) async-start(), calls=%async_computation.28 | async-start | bytes 2457600 | tf_op jit(solution)/shard_map/all_gather | solution.py:177
  225.1 508.4 %all-gather.23.cloned.1.call-start = ((), (), s32[]{:S(2)}) async-start(), calls=%async_computation.24 | async-start | bytes 2457600 | tf_op jit(solution)/shard_map/all_gather | solution.py:177
  225.7 766.2 %reduce-scatter.45.cloned.1.call-start = ((), (), s32[]{:S(2)}) async-start(), calls=%async_computation.37 | async-start | bytes 614400
  226.6 116.7 %copy-start.107 = (s32[1600]{0:T(1024)}, s32[1600]{0:T(1024)S(1)}, u32[]{:S(2)}) copy-start(s32[1600]{0:T(1024)S(1)} %get-tuple-element.88) | copy-start | bytes 19204
  226.6 116.7 %copy-start.109 = (s32[1600]{0:T(1024)}, s32[1600]{0:T(1024)S(1)}, u32[]{:S(2)}) copy-start(s32[1600]{0:T(1024)S(1)} %get-tuple-element.89) | copy-start | bytes 19204
  305.9 37.5 %copy-start.46 = (bf16[1600,512]{1,0:T(8,128)(2,1)S(1)}, bf16[1600,512]{1,0:T(8,128)(2,1)}, u32[]{:S(2)}) copy-start(bf16[1600,512]{1,0:T(8,128)(2,1)} %all-gather.13.cloned.1.call-done) | copy-start | bytes 4915204
  690.5 304.4 %reduce-scatter.43.cloned.1.call-start = ((), (), s32[]{:S(2)}) async-start(), calls=%async_computation.36 | async-start | bytes 614400
  711.3 22.3 %copy-start.110 = (s32[1600]{0:T(1024)S(1)}, s32[1600]{0:T(1024)}, u32[]{:S(2)}) copy-start(s32[1600]{0:T(1024)} %copy-done.109) | copy-start | bytes 19204
  844.3 157.5 %reduce-scatter.27.cloned.1.call-start = ((), (), s32[]{:S(2)}) async-start(), calls=%async_computation.25 | async-start | bytes 2457600 | tf_op jit(solution)/shard_map/reduce_scatter | solution.py:207
  848.1 157.8 %reduce-scatter.31.cloned.1.call-start = ((), (), s32[]{:S(2)}) async-start(), calls=%async_computation.29 | async-start | bytes 2457600 | tf_op jit(solution)/shard_map/reduce_scatter | solution.py:207
  923.0 88.9 %reduce-scatter.25.cloned.1.call-start = ((), (), s32[]{:S(2)}) async-start(), calls=%async_computation.23 | async-start | bytes 2457600 | tf_op jit(solution)/shard_map/reduce_scatter | solution.py:164
  953.2 58.8 %reduce-scatter.21.cloned.1.call-start = ((), (), s32[]{:S(2)}) async-start(), calls=%async_computation.19 | async-start | bytes 2457600 | tf_op jit(solution)/shard_map/reduce_scatter | solution.py:164
  983.0 64.4 %all-gather.25.cloned.1.call-start = ((), (), s32[]{:S(2)}) async-start(), calls=%async_computation.26 | async-start | bytes 2457600 | tf_op jit(solution)/shard_map/all_gather | solution.py:231
  987.3 24.6 %copy-start.64 = (f32[800]{0:T(1024)}, f32[800]{0:T(1024)S(1)}, u32[]{:S(2)}) copy-start(f32[800]{0:T(1024)S(1)} %get-tuple-element.169) | copy-start | bytes 9604
  1017.4 30.0 %copy-start.28 = (bf16[256,512]{0,1:T(8,128)(2,1)S(1)}, bf16[256,512]{0,1:T(8,128)(2,1)}, u32[]{:S(2)}) copy-start(bf16[256,512]{0,1:T(8,128)(2,1)} %copy-done.27) | copy-start | bytes 786436
  1019.6 57.8 %all-gather.29.cloned.1.call-start = ((), (), s32[]{:S(2)}) async-start(), calls=%async_computation.30 | async-start | bytes 2457600 | tf_op jit(solution)/shard_map/all_gather | solution.py:231
  1020.1 267.6 %all-reduce.17.cloned.1.call-start = ((), (), s32[]{:S(2)}) async-start(), calls=%async_computation.38 | async-start | bytes 2097152
  1131.3 157.9 %reduce-scatter.35.cloned.1.call-start = ((), (), s32[]{:S(2)}) async-start(), calls=%async_computation.32 | async-start | bytes 278528 | tf_op jit(solution)/shard_map/reduce_scatter | solution.py:288
  1135.3 176.4 %reduce-scatter.29.cloned.1.call-start = ((), (), s32[]{:S(2)}) async-start(), calls=%async_computation.27 | async-start | bytes 2457600 | tf_op jit(solution)/shard_map/reduce_scatter | solution.py:267
  1139.8 30.3 %copy-start.40 = (bf16[1600,768]{0,1:T(8,128)(2,1)S(1)}, bf16[1600,768]{0,1:T(8,128)(2,1)}, u32[]{:S(2)}) copy-start(bf16[1600,768]{0,1:T(8,128)(2,1)} %reshape.490) | copy-start | bytes 7372804
  1139.9 201.6 %reduce-scatter.33.cloned.1.call-start = ((), (), s32[]{:S(2)}) async-start(), calls=%async_computation.31 | async-start | bytes 2457600 | tf_op jit(solution)/shard_map/reduce_scatter | solution.py:267
  1172.8 503.4 %reduce-scatter.41.cloned.1.call-start = ((), (), s32[]{:S(2)}) async-start(), calls=%async_computation.35 | async-start | bytes 35651584 | tf_op jit(solution)/shard_map/reduce_scatter | solution.py:294
  1213.4 796.7 %reduce-scatter.39.cloned.1.call-start = ((), (), s32[]{:S(2)}) async-start(), calls=%async_computation.34 | async-start | bytes 35651584 | tf_op jit(solution)/shard_map/reduce_scatter | solution.py:291
  1278.7 868.9 %reduce-scatter.37.cloned.1.call-start = ((), (), s32[]{:S(2)}) async-start(), calls=%async_computation.33 | async-start | bytes 270336 | tf_op jit(solution)/shard_map/reduce_scatter | solution.py:303
  1283.5 57.9 %copy-start.3 = (f32[2,800,512]{2,1,0:T(8,128)S(1)}, f32[2,800,512]{2,1,0:T(8,128)}, u32[]{:S(2)}) copy-start(f32[2,800,512]{2,1,0:T(8,128)} %param.14) | copy-start | bytes 9830404
  1283.5 57.9 %copy-start.54 = (f32[800]{0:T(1024)S(1)}, f32[800]{0:T(1024)}, u32[]{:S(2)}) copy-start(f32[800]{0:T(1024)} %copy-done.53) | copy-start | bytes 9604
  1283.6 57.9 %copy-start.56 = (f32[800]{0:T(1024)S(1)}, f32[800]{0:T(1024)}, u32[]{:S(2)}) copy-start(f32[800]{0:T(1024)} %copy-done.55) | copy-start | bytes 9604
  1283.6 57.9 %copy-start.97 = (f32[512]{0:T(512)S(1)}, f32[512]{0:T(512)}, u32[]{:S(2)}) copy-start(f32[512]{0:T(512)} %copy-done.96) | copy-start | bytes 6148
  1287.7 56.4 %copy-start.91 = (f32[800]{0:T(1024)S(1)}, f32[800]{0:T(1024)}, u32[]{:S(2)}) copy-start(f32[800]{0:T(1024)} %copy-done.90) | copy-start | bytes 9604
  1287.7 56.5 %copy-start.89 = (f32[800]{0:T(1024)S(1)}, f32[800]{0:T(1024)}, u32[]{:S(2)}) copy-start(f32[800]{0:T(1024)} %copy-done.88) | copy-start | bytes 9604
  1287.7 56.5 %copy-start.77 = (f32[800]{0:T(1024)S(1)}, f32[800]{0:T(1024)}, u32[]{:S(2)}) copy-start(f32[800]{0:T(1024)} %copy-done.76) | copy-start | bytes 9604
  1287.7 56.5 %copy-start.79 = (f32[800]{0:T(1024)S(1)}, f32[800]{0:T(1024)}, u32[]{:S(2)}) copy-start(f32[800]{0:T(1024)} %copy-done.78) | copy-start | bytes 9604
  1344.1 43.5 %copy-start.85 = (f32[800]{0:T(1024)S(1)}, f32[800]{0:T(1024)}, u32[]{:S(2)}) copy-start(f32[800]{0:T(1024)} %copy-done.84) | copy-start | bytes 9604
  1344.1 43.4 %copy-start.87 = (f32[800]{0:T(1024)S(1)}, f32[800]{0:T(1024)}, u32[]{:S(2)}) copy-start(f32[800]{0:T(1024)} %copy-done.86) | copy-start | bytes 9604
  (98 other events, 489.9 us)
Sparse Core Ops, SparseCore 0:
  56.1 27.7 all-gather.10
  86.0 27.9 all-gather.18
  146.6 24.4 reduce-scatter.18
  190.6 24.4 reduce-scatter.22
  221.7 29.6 all-gather.20
  252.8 29.5 all-gather.12
  284.0 168.2 all-gather.14
  453.8 168.0 all-gather.16
  624.0 27.8 all-gather.26
  653.3 27.9 all-gather.22
  690.6 13.3 reduce-scatter.44
  844.5 13.3 reduce-scatter.42
  860.1 26.8 reduce-scatter.26
  923.1 26.7 reduce-scatter.30
  953.3 26.7 reduce-scatter.24
  983.1 26.7 reduce-scatter.20
  1019.7 27.7 all-gather.24
  1049.4 27.9 all-gather.28
  1131.5 93.7 all-reduce.16
  1228.6 54.8 reduce-scatter.34
  1285.7 25.9 reduce-scatter.28
  1314.5 26.8 reduce-scatter.32
  1345.7 330.5 reduce-scatter.40
  1680.4 329.6 reduce-scatter.38
  2012.8 134.7 reduce-scatter.36
where the time goes:
time: 2160 us; the launch traced here: 2150 us
  waiting for transfers between devices  1100 us (51%)
  matrix products  465 us (22%)
  local copies, waits for them, and re-layouts  293 us (14%)
  blocking collectives  194 us (9%)
  other arithmetic  82 us (4%)
    reduce_scatter x1, waiting for transfers between devices, per_device(): lax.psum_scatter(first_acc.astype(jnp.bfloat16), 'dp', scatter_dimension=...  330 us
    reduce_scatter x1, waiting for transfers between devices, per_device(): lax.psum_scatter(second_acc.astype(jnp.bfloat16), 'dp', scatter_dimension...  281 us
    all_gather x1, waiting for transfers between devices, current_weights(): lax.all_gather(expert_out, 'dp', axis=2, tiled=True)  148 us
    reduce_scatter x1, waiting for transfers between devices, per_device(): lax.psum_scatter(router_acc, ('dp', 'tensor'), scatter_dimension=0, tiled...  133 us
    all_gather x1, waiting for transfers between devices, current_weights(): lax.all_gather(expert_in, 'dp', axis=1, tiled=True)  87.7 us
    unnamed x2, blocking collectives  81.4 us
    dot_general x2, matrix products, per_device(): jnp.einsum('ecf,ecd->efd', hidden, result_grad, preferred_element_type=jn...  70.7 us
    all_gather x1, blocking collectives, per_device(): lax.all_gather(router_weight, ('dp', 'tensor'), axis=0, tiled=True)  69.3 us
  transfers between devices with their start and end apart: 25, of which 11 were waited for; matrix products, arithmetic and copies ran while one was open for 35% of the time, Pallas kernels for 0%

commit v1 on v0

--- a/solution.py
+++ b/solution.py
@@ -2,12 +2,36 @@
 import jax.numpy as jnp
 from jax import lax
 from jax.sharding import PartitionSpec as P
+from jax.lax import axis_index, axis_size, ppermute
 
 HEAD = 64
 CAP = 120
 EPSILON = 1e-06
 FIRST_DIMS = (((0,), (0,)), ((), ()))
 LAST_DIMS = (((1,), (1,)), ((), ()))
+
+
+def deliver_the_packet(z, bus_axis):
+    oldest = axis_size(bus_axis)
+    seen_now = axis_index(bus_axis)
+    taken_in, block_out, side_arr = (oldest, seen_now, z.shape[2])
+    pages = [(h, (h + 1) % taken_in) for h in range(taken_in)]
+    arrivals = [(h, (h - 1) % taken_in) for h in range(taken_in)]
+    part_now = jnp.zeros((*z.shape[:2], taken_in * side_arr, *z.shape[3:]), z.dtype)
+    part_now = lax.dynamic_update_slice_in_dim(part_now, z, block_out * side_arr, axis=2)
+    response = after = z
+    m_next = taken_in // 2
+    for pp in [*range(1, m_next + 1)]:
+        response = ppermute(response, bus_axis, pages)
+        part_now = lax.dynamic_update_slice_in_dim(
+            part_now, response, (block_out - pp) % taken_in * side_arr, axis=2
+        )
+        if pp < taken_in - m_next:
+            after = ppermute(after, bus_axis, arrivals)
+            part_now = lax.dynamic_update_slice_in_dim(
+                part_now, after, (block_out + pp) % taken_in * side_arr, axis=2
+            )
+    return part_now
 
 
 def norm_rows(values, gain, offset):
@@ -71,7 +95,7 @@
             fetch_attention(),
             (
                 lax.all_gather(expert_in, "dp", axis=1, tiled=True),
-                lax.all_gather(expert_out, "dp", axis=2, tiled=True),
+                deliver_the_packet(expert_out, "dp"),
             ),
         )
 

time: 2160 us -> 3910 us (1.81); the launches traced: 2150 us -> 3860 us
  local copies, waits for them, and re-layouts: 293 us -> 1830 us
  starting transfers between devices: 1.58 us -> 338 us
  waiting for transfers between devices: 1100 us -> 918 us
    dynamic_update_slice x0 -> x16, local copies, waits for them, and re-layouts: none -> 1410 us  [the longest x8 700 us: deliver_the_packet(): lax.dynamic_update_slice_in_dim(part_now, response, (block_out - pp) % ta...]
    ppermute x0 -> x15, starting transfers between devices: none -> 336 us  [the longest x8 327 us: deliver_the_packet(): response = ppermute(response, bus_axis, pages)]
    all_gather x1 -> x0, waiting for transfers between devices: 148 us -> none  [current_weights(): lax.all_gather(expert_out, 'dp', axis=2, tiled=True)]
    ppermute x0 -> x15, local copies, waits for them, and re-layouts: none -> 115 us  [the longest x8 62.7 us: deliver_the_packet(): response = ppermute(response, bus_axis, pages)]
    all_gather x1, waiting for transfers between devices: 87.7 us -> 0.01 us  [current_weights(): lax.all_gather(expert_in, 'dp', axis=1, tiled=True)]
    ppermute x0 -> x15, waiting for transfers between devices: none -> 49.3 us  [the longest x8 38.8 us: deliver_the_packet(): response = ppermute(response, bus_axis, pages)]
    reduce_scatter x1, waiting for transfers between devices: 281 us -> 330 us  [per_device(): lax.psum_scatter(second_acc.astype(jnp.bfloat16), 'dp', scatter_dimension...]
    reduce_scatter x1, waiting for transfers between devices: 330 us -> 281 us  [per_device(): lax.psum_scatter(first_acc.astype(jnp.bfloat16), 'dp', scatter_dimension=...]
  transfers between devices with their start and end apart: 25 -> 39, of which waited for: 11 -> 15; matrix products, arithmetic and copies ran while one was open for 35% -> 60% of each run, Pallas kernels for 0% -> 0%
where the time goes in v1:
time: 3910 us; the launch traced here: 3860 us
  local copies, waits for them, and re-layouts  1830 us (47%)
  waiting for transfers between devices  918 us (23%)
  matrix products  464 us (12%)
  starting transfers between devices  338 us (9%)
  blocking collectives  210 us (5%)
  other arithmetic  82.4 us (2%)
    dynamic_update_slice x8, local copies, waits for them, and re-layouts, deliver_the_packet(): lax.dynamic_update_slice_in_dim(part_now, response, (block_out - pp) % ta...  700 us
    dynamic_update_slice x7, local copies, waits for them, and re-layouts, deliver_the_packet(): lax.dynamic_update_slice_in_dim(part_now, after, (block_out + pp) % taken...  629 us
    reduce_scatter x1, waiting for transfers between devices, per_device(): lax.psum_scatter(second_acc.astype(jnp.bfloat16), 'dp', scatter_dimension...  330 us
    ppermute x8, starting transfers between devices, deliver_the_packet(): response = ppermute(response, bus_axis, pages)  327 us
    reduce_scatter x1, waiting for transfers between devices, per_device(): lax.psum_scatter(first_acc.astype(jnp.bfloat16), 'dp', scatter_dimension=...  281 us
    reduce_scatter x1, waiting for transfers between devices, per_device(): lax.psum_scatter(router_acc, ('dp', 'tensor'), scatter_dimension=0, tiled...  133 us
    all_gather x1, blocking collectives, per_device(): lax.all_gather(router_weight, ('dp', 'tensor'), axis=0, tiled=True)  85.6 us
    unnamed x2, blocking collectives  81.4 us
  transfers between devices with their start and end apart: 39, of which 15 were waited for; matrix products, arithmetic and copies ran while one was open for 60% of the time, Pallas kernels for 0%

profile of v1, /device:TPU:0, one launch (start us, length us, event | category | flops | bytes accessed | tf_op | source)
XLA Modules:
  0.0 3864.5 jit_solution(1955664422981135792)
XLA Ops:
  12.3 42.0 %all-reduce.14 = (f32[512]{0:T(512)S(1)}, f32[512]{0:T(512)S(1)}, f32[512]{0:T(512)S(1)}, f32[512]{0:T(512)S(1)}) all-reduce(f32[512]{0:T(512)S(1)} %dynamic-update-slice.1, f32[512]{0:T(512)S(1)} %dynamic-update-slice, f32[512]{0:T(512)S(1)} %dynamic-update-slice.3, ...), channel_id=1, replica_groups=mesh['dp'=16,'tensor'=2] {'dp','tensor'}, use_global_device_ids=true, to_apply=%add.5 | all-reduce | flops 2048 | bytes 16384
  56.8 24.6 all_gather.60
  83.8 18.6 all_gather.61
  190.3 24.5 reduce-scatter.23.cloned.1.call-done
  226.9 24.0 collective-permute-done
  251.0 18.9 collective-permute-start.2
  279.2 102.0 %collective-permute-start.4 = (bf16[32,1024,32]{1,2,0:T(8,128)(2,1)S(1)}, bf16[32,1024,32]{1,2,0:T(8,128)(2,1)}, u32[]{:S(2)}, u32[]{:S(2)}) collective-permute-start(bf16[32,1024,32]{1,2,0:T(8,128)(2,1)S(1)} %collective-permute-done.2), channel_id=1, source_target_pairs={{0,2},{2,4},{4,6},{6,8},{8,10},{10,12},{12,14},{14,16},{16,18},{18... | collective-permute-start | bytes 6291464 | tf_op jit(solution)/shard_map/ppermute | solution.py:25
  385.2 89.2 %collective-permute-start.6 = (bf16[32,1024,32]{1,2,0:T(8,128)(2,1)}, bf16[32,1024,32]{1,2,0:T(8,128)(2,1)}, u32[]{:S(2)}, u32[]{:S(2)}) collective-permute-start(bf16[32,1024,32]{1,2,0:T(8,128)(2,1)} %collective-permute-done.4), channel_id=1, source_target_pairs={{0,2},{2,4},{4,6},{6,8},{8,10},{10,12},{12,14},{14,16},{16,18},{18... | collective-permute-start | bytes 6291464 | tf_op jit(solution)/shard_map/ppermute | solution.py:25
  478.5 67.4 %collective-permute-start.8 = (bf16[32,1024,32]{1,2,0:T(8,128)(2,1)}, bf16[32,1024,32]{1,2,0:T(8,128)(2,1)}, u32[]{:S(2)}, u32[]{:S(2)}) collective-permute-start(bf16[32,1024,32]{1,2,0:T(8,128)(2,1)} %collective-permute-done.6), channel_id=1, source_target_pairs={{0,2},{2,4},{4,6},{6,8},{8,10},{10,12},{12,14},{14,16},{16,18},{18... | collective-permute-start | bytes 6291464 | tf_op jit(solution)/shard_map/ppermute | solution.py:25
  569.8 78.8 %dynamic_update_slice.32 = bf16[32,1024,512]{2,1,0:T(8,128)(2,1)} dynamic-update-slice(bf16[32,1024,512]{2,1,0:T(8,128)(2,1)} %broadcast.465, bf16[32,1024,32]{2,1,0:T(8,128)(2,1)} %copy.301, s32[]{:T(128)} %constant.236.clone.1, s32[]{:T(128)} %constant.236.clone.1, s32[]{:T(128)S(6)} %select_n.395) | dynamic-update-slice | bytes 4194308 | tf_op jit(solution)/shard_map/dynamic_update_slice | solution.py:21
  667.1 85.6 %all_gather.65 = f32[512,32]{1,0:T(8,128)S(1)} all-gather(f32[16,32]{1,0:T(8,128)S(1)} %copy-done.110), channel_id=1, replica_groups=mesh['dp'=16,'tensor'=2] {'dp','tensor'}, dimensions={0}, use_global_device_ids=true | all-gather | bytes 67584 | tf_op jit(solution)/shard_map/all_gather | solution.py:72
  761.2 90.0 %dynamic_update_slice.33 = bf16[32,1024,512]{2,1,0:T(8,128)(2,1)} dynamic-update-slice(bf16[32,1024,512]{2,1,0:T(8,128)(2,1)} %dynamic_update_slice.32, bf16[32,1024,32]{2,1,0:T(8,128)(2,1)} %copy.302, s32[]{:T(128)} %constant.236.clone.1, s32[]{:T(128)} %constant.236.clone.1, s32[]{:T(128)S(6)} %select_n.397) | dynamic-update-slice | bytes 4194308 | tf_op jit(solution)/shard_map/dynamic_update_slice | solution.py:26
  859.0 91.7 %dynamic_update_slice.34 = bf16[32,1024,512]{2,1,0:T(8,128)(2,1)} dynamic-update-slice(bf16[32,1024,512]{2,1,0:T(8,128)(2,1)} %dynamic_update_slice.33, bf16[32,1024,32]{2,1,0:T(8,128)(2,1)} %copy.303, s32[]{:T(128)} %constant.236.clone.1, s32[]{:T(128)} %constant.236.clone.1, s32[]{:T(128)S(6)} %select_n.399) | dynamic-update-slice | bytes 4194308 | tf_op jit(solution)/shard_map/dynamic_update_slice | solution.py:31
  958.4 90.0 %dynamic_update_slice.35 = bf16[32,1024,512]{2,1,0:T(8,128)(2,1)} dynamic-update-slice(bf16[32,1024,512]{2,1,0:T(8,128)(2,1)} %dynamic_update_slice.34, bf16[32,1024,32]{2,1,0:T(8,128)(2,1)} %copy.304, s32[]{:T(128)} %constant.236.clone.1, s32[]{:T(128)} %constant.236.clone.1, s32[]{:T(128)S(6)} %select_n.401) | dynamic-update-slice | bytes 4194308 | tf_op jit(solution)/shard_map/dynamic_update_slice | solution.py:26
  1056.2 91.7 %dynamic_update_slice.36 = bf16[32,1024,512]{2,1,0:T(8,128)(2,1)} dynamic-update-slice(bf16[32,1024,512]{2,1,0:T(8,128)(2,1)} %dynamic_update_slice.35, bf16[32,1024,32]{2,1,0:T(8,128)(2,1)} %copy.305, s32[]{:T(128)} %constant.236.clone.1, s32[]{:T(128)} %constant.236.clone.1, s32[]{:T(128)S(6)} %select_n.403) | dynamic-update-slice | bytes 4194308 | tf_op jit(solution)/shard_map/dynamic_update_slice | solution.py:31
  1155.7 90.0 %dynamic_update_slice.37 = bf16[32,1024,512]{2,1,0:T(8,128)(2,1)} dynamic-update-slice(bf16[32,1024,512]{2,1,0:T(8,128)(2,1)} %dynamic_update_slice.36, bf16[32,1024,32]{2,1,0:T(8,128)(2,1)} %copy.306, s32[]{:T(128)} %constant.236.clone.1, s32[]{:T(128)} %constant.236.clone.1, s32[]{:T(128)S(6)} %select_n.405) | dynamic-update-slice | bytes 4194308 | tf_op jit(solution)/shard_map/dynamic_update_slice | solution.py:26
  1253.5 91.7 %dynamic_update_slice.38 = bf16[32,1024,512]{2,1,0:T(8,128)(2,1)} dynamic-update-slice(bf16[32,1024,512]{2,1,0:T(8,128)(2,1)} %dynamic_update_slice.37, bf16[32,1024,32]{2,1,0:T(8,128)(2,1)} %copy.307, s32[]{:T(128)} %constant.236.clone.1, s32[]{:T(128)} %constant.236.clone.1, s32[]{:T(128)S(6)} %select_n.407) | dynamic-update-slice | bytes 4194308 | tf_op jit(solution)/shard_map/dynamic_update_slice | solution.py:31
  1380.8 32.5 collective-permute-start.14
  1465.8 76.5 %dynamic_update_slice.39 = bf16[32,1024,512]{2,1,0:T(8,128)(2,1)} dynamic-update-slice(bf16[32,1024,512]{2,1,0:T(8,128)(2,1)} %dynamic_update_slice.38, bf16[32,1024,32]{2,1,0:T(8,128)(2,1)} %copy.308, s32[]{:T(128)} %constant.236.clone.1, s32[]{:T(128)} %constant.236.clone.1, s32[]{:T(128)S(6)} %select_n.409) | dynamic-update-slice | bytes 4194308 | tf_op jit(solution)/shard_map/dynamic_update_slice | solution.py:26
  1548.2 78.6 %dynamic_update_slice.40 = bf16[32,1024,512]{2,1,0:T(8,128)(2,1)} dynamic-update-slice(bf16[32,1024,512]{2,1,0:T(8,128)(2,1)} %dynamic_update_slice.39, bf16[32,1024,32]{2,1,0:T(8,128)(2,1)} %copy.309, s32[]{:T(128)} %constant.236.clone.1, s32[]{:T(128)} %constant.236.clone.1, s32[]{:T(128)S(6)} %select_n.411) | dynamic-update-slice | bytes 4194308 | tf_op jit(solution)/shard_map/dynamic_update_slice | solution.py:31
  1634.6 91.6 %dynamic_update_slice.41 = bf16[32,1024,512]{2,1,0:T(8,128)(2,1)} dynamic-update-slice(bf16[32,1024,512]{2,1,0:T(8,128)(2,1)} %dynamic_update_slice.40, bf16[32,1024,32]{2,1,0:T(8,128)(2,1)} %copy.310, s32[]{:T(128)} %constant.236.clone.1, s32[]{:T(128)} %constant.236.clone.1, s32[]{:T(128)S(6)} %select_n.413) | dynamic-update-slice | bytes 4194308 | tf_op jit(solution)/shard_map/dynamic_update_slice | solution.py:26
  1734.0 91.6 %dynamic_update_slice.42 = bf16[32,1024,512]{2,1,0:T(8,128)(2,1)} dynamic-update-slice(bf16[32,1024,512]{2,1,0:T(8,128)(2,1)} %dynamic_update_slice.41, bf16[32,1024,32]{2,1,0:T(8,128)(2,1)} %copy.311, s32[]{:T(128)} %constant.236.clone.1, s32[]{:T(128)} %constant.236.clone.1, s32[]{:T(128)S(6)} %select_n.415) | dynamic-update-slice | bytes 4194308 | tf_op jit(solution)/shard_map/dynamic_update_slice | solution.py:31
  1833.4 91.6 %dynamic_update_slice.43 = bf16[32,1024,512]{2,1,0:T(8,128)(2,1)} dynamic-update-slice(bf16[32,1024,512]{2,1,0:T(8,128)(2,1)} %dynamic_update_slice.42, bf16[32,1024,32]{2,1,0:T(8,128)(2,1)} %copy.312, s32[]{:T(128)} %constant.236.clone.1, s32[]{:T(128)} %constant.236.clone.1, s32[]{:T(128)S(6)} %select_n.417) | dynamic-update-slice | bytes 4194308 | tf_op jit(solution)/shard_map/dynamic_update_slice | solution.py:26
  1932.9 91.6 %dynamic_update_slice.44 = bf16[32,1024,512]{2,1,0:T(8,128)(2,1)} dynamic-update-slice(bf16[32,1024,512]{2,1,0:T(8,128)(2,1)} %dynamic_update_slice.43, bf16[32,1024,32]{2,1,0:T(8,128)(2,1)} %copy.313, s32[]{:T(128)} %constant.236.clone.1, s32[]{:T(128)} %constant.236.clone.1, s32[]{:T(128)S(6)} %select_n.419) | dynamic-update-slice | bytes 4194308 | tf_op jit(solution)/shard_map/dynamic_update_slice | solution.py:31
  2032.3 91.6 %dynamic_update_slice.45 = bf16[32,1024,512]{2,1,0:T(8,128)(2,1)} dynamic-update-slice(bf16[32,1024,512]{2,1,0:T(8,128)(2,1)} %dynamic_update_slice.44, bf16[32,1024,32]{2,1,0:T(8,128)(2,1)} %copy.314, s32[]{:T(128)} %constant.236.clone.1, s32[]{:T(128)} %constant.236.clone.1, s32[]{:T(128)S(6)} %select_n.421) | dynamic-update-slice | bytes 4194308 | tf_op jit(solution)/shard_map/dynamic_update_slice | solution.py:26
  2131.7 91.6 %dynamic_update_slice.46 = bf16[32,1024,512]{2,1,0:T(8,128)(2,1)} dynamic-update-slice(bf16[32,1024,512]{2,1,0:T(8,128)(2,1)} %dynamic_update_slice.45, bf16[32,1024,32]{2,1,0:T(8,128)(2,1)} %copy.315, s32[]{:T(128)} %constant.236.clone.1, s32[]{:T(128)} %constant.236.clone.1, s32[]{:T(128)S(6)} %select_n.423) | dynamic-update-slice | bytes 4194308 | tf_op jit(solution)/shard_map/dynamic_update_slice | solution.py:31
  2231.2 78.5 %dynamic_update_slice.47 = bf16[32,1024,512]{2,1,0:T(8,128)(2,1)} dynamic-update-slice(bf16[32,1024,512]{2,1,0:T(8,128)(2,1)} %dynamic_update_slice.46, bf16[32,1024,32]{2,1,0:T(8,128)(2,1)} %copy.316, s32[]{:T(128)} %constant.236.clone.1, s32[]{:T(128)} %constant.236.clone.1, s32[]{:T(128)S(6)} %select_n.425) | dynamic-update-slice | bytes 4194308 | tf_op jit(solution)/shard_map/dynamic_update_slice | solution.py:26
  2309.7 20.1 fusion.144
  2329.8 21.2 fusion.129
  2369.0 24.3 fusion.16
  2393.3 19.2 gather_fusion.6
  2414.1 20.1 fusion.145
  2434.2 21.1 fusion.130
  2473.8 24.3 fusion.23
  2498.1 21.0 fusion.146
  2544.9 19.1 gather_fusion.9
  2569.5 21.2 fusion.147
  2728.3 29.2 all-gather.22.cloned.1.call-done
  2849.7 27.9 fusion.150
  2880.3 38.0 add_convert_fusion.1
  2918.4 30.0 fusion.128
  2948.4 40.3 %add_convert_fusion = bf16[32,1024,512]{1,2,0:T(8,128)(2,1)} fusion(f32[32,1024,512]{1,2,0:T(8,128)} %fusion.128, bf16[32,120,512]{2,1,0:T(8,128)(2,1)} %bitcast.287, f32[32,120,1024]{2,1,0:T(8,128)} %fusion.145), kind=kOutput, calls=%fused_computation.12 | convolution fusion | flops 4095475712 | bytes 120324096 | tf_op jit(solution)/shard_map/ecf,ecd->efd/dot_general | solution.py:218
  3000.8 20.7 reduce-scatter.29.cloned.1.call-done
  3021.5 29.7 reduce-scatter.33.cloned.1.call-done
  3055.7 39.4 %all-reduce.13 = (f32[512]{0:T(512)S(1)}, f32[512]{0:T(512)S(1)}, f32[512]{0:T(512)S(1)}, f32[512]{0:T(512)S(1)}) all-reduce(f32[512]{0:T(512)S(1)} %add.647, f32[512]{0:T(512)S(1)} %add.648, f32[512]{0:T(512)S(1)} %add.651, f32[512]{0:T(512)S(1)} %add.652), channel_id=12, replica_groups=mesh['dp'=16,'tensor'=2] {'dp','tensor'}, use_global_device_ids=true, to_apply=%region_52.53.clone | all-reduce | flops 2048 | bytes 16384
  3104.9 281.1 %reduce-scatter.39.cloned.1.call-done = bf16[32,32,1024]{2,1,0:T(8,128)(2,1)} async-done(((bf16[32,512,1024]{2,1,0:T(8,128)(2,1)}), bf16[32,32,1024]{2,1,0:T(8,128)(2,1)}) %reduce-scatter.39.cloned.1.call-update) | async-done | bytes 2097168 | tf_op jit(solution)/shard_map/reduce_scatter | solution.py:315
  3390.1 329.9 %reduce-scatter.41.cloned.1.call-done = bf16[32,1024,32]{1,2,0:T(8,128)(2,1)} async-done(((bf16[32,1024,512]{1,2,0:T(8,128)(2,1)}), bf16[32,1024,32]{1,2,0:T(8,128)(2,1)}) %reduce-scatter.41.cloned.1.call-update) | async-done | bytes 2097168 | tf_op jit(solution)/shard_map/reduce_scatter | solution.py:318
  3724.1 133.3 %reduce-scatter.37.cloned.1.call-done = f32[16,32]{1,0:T(8,128)} async-done(((f32[512,32]{1,0:T(8,128)}), f32[16,32]{1,0:T(8,128)}) %reduce-scatter.37.cloned.1.call-update) | async-done | bytes 2064 | tf_op jit(solution)/shard_map/reduce_scatter | solution.py:327
  (549 shorter events, 699.5 us)
Async XLA Ops:
  7.2 95.1 %all-gather.10.cloned.1.call-start = ((), (), s32[]{:S(2)}) async-start(), calls=%async_computation.14 | async-start | bytes 2457600 | tf_op jit(solution)/shard_map/all_gather | solution.py:133
  54.3 164.6 %copy-start.103 = (f32[512]{0:T(512)}, f32[512]{0:T(512)S(1)}, u32[]{:S(2)}) copy-start(f32[512]{0:T(512)S(1)} %get-tuple-element.101) | copy-start | bytes 6148
  56.0 90.5 %all-gather.16.cloned.1.call-start = ((), (), s32[]{:S(2)}) async-start(), calls=%async_computation.19 | async-start | bytes 2457600 | tf_op jit(solution)/shard_map/all_gather | solution.py:133
  56.8 133.5 %reduce-scatter.19.cloned.1.call-start = ((), (), s32[]{:S(2)}) async-start(), calls=%async_computation.15 | async-start | bytes 2457600 | tf_op jit(solution)/shard_map/reduce_scatter | solution.py:152
  102.3 84.9 %copy-start.27 = (bf16[256,512]{0,1:T(8,128)(2,1)}, bf16[256,512]{0,1:T(8,128)(2,1)S(1)}, u32[]{:S(2)}) copy-start(bf16[256,512]{0,1:T(8,128)(2,1)S(1)} %all_gather.61) | copy-start | bytes 786436
  146.2 68.6 %reduce-scatter.23.cloned.1.call-start = ((), (), s32[]{:S(2)}) async-start(), calls=%async_computation.20 | async-start | bytes 2457600 | tf_op jit(solution)/shard_map/reduce_scatter | solution.py:152
  190.2 1154.9 %all-gather.12.cloned.1.call-start = ((), (), s32[]{:S(2)}) async-start(), calls=%async_computation.16 | async-start | bytes 2457600 | tf_op jit(solution)/shard_map/all_gather | solution.py:159
  218.9 255.5 %copy-start.10 = (f32[2,800,512]{2,1,0:T(8,128)S(1)}, f32[2,800,512]{2,1,0:T(8,128)}, u32[]{:S(2)}) copy-start(f32[2,800,512]{2,1,0:T(8,128)} %param.27) | copy-start | bytes 9830404
  220.6 1128.4 %all-gather.18.cloned.1.call-start = ((), (), s32[]{:S(2)}) async-start(), calls=%async_computation.21 | async-start | bytes 2457600 | tf_op jit(solution)/shard_map/all_gather | solution.py:159
  221.2 2088.5 %all-gather.14.cloned.1.call-start = ((), (), s32[]{:S(2)}) async-start(), calls=%async_computation.17 | async-start | bytes 35651584 | tf_op jit(solution)/shard_map/all_gather | solution.py:97
  221.9 2129.2 %all-gather.20.cloned.1.call-start = ((), (), s32[]{:S(2)}) async-start(), calls=%async_computation.23 | async-start | bytes 2457600 | tf_op jit(solution)/shard_map/all_gather | solution.py:201
  222.0 29.0 collective-permute-start
  222.5 47.3 %collective-permute-start.1 = (bf16[32,1024,32]{1,2,0:T(8,128)(2,1)}, bf16[32,1024,32]{1,2,0:T(8,128)(2,1)S(1)}, u32[]{:S(2)}, u32[]{:S(2)}) collective-permute-start(bf16[32,1024,32]{1,2,0:T(8,128)(2,1)} %param.26), channel_id=1, source_target_pairs={{0,30},{2,0},{4,2},{6,4},{8,6},{10,8},{12,10},{14,12},{16,14},{18,... | collective-permute-start | bytes 6291464 | tf_op jit(solution)/shard_map/ppermute | solution.py:30
  251.0 134.2 %copy-start.43 = (bf16[32,1024,32]{1,2,0:T(8,128)(2,1)}, bf16[32,1024,32]{1,2,0:T(8,128)(2,1)S(1)}, u32[]{:S(2)}) copy-start(bf16[32,1024,32]{1,2,0:T(8,128)(2,1)S(1)} %collective-permute-done) | copy-start | bytes 6291460
  251.0 28.3 collective-permute-start.2
  271.2 110.1 %collective-permute-start.3 = (bf16[32,1024,32]{1,2,0:T(8,128)(2,1)S(1)}, bf16[32,1024,32]{1,2,0:T(8,128)(2,1)}, u32[]{:S(2)}, u32[]{:S(2)}) collective-permute-start(bf16[32,1024,32]{1,2,0:T(8,128)(2,1)S(1)} %collective-permute-done.1), channel_id=1, source_target_pairs={{0,30},{2,0},{4,2},{6,4},{8,6},{10,8},{12,10},{14,12},{16,14},{18,... | collective-permute-start | bytes 6291464 | tf_op jit(solution)/shard_map/ppermute | solution.py:30
  279.2 102.0 %copy-start.42 = (bf16[32,1024,32]{1,2,0:T(8,128)(2,1)}, bf16[32,1024,32]{1,2,0:T(8,128)(2,1)S(1)}, u32[]{:S(2)}) copy-start(bf16[32,1024,32]{1,2,0:T(8,128)(2,1)S(1)} %collective-permute-done.2) | copy-start | bytes 6291460
  279.2 105.9 %collective-permute-start.4 = (bf16[32,1024,32]{1,2,0:T(8,128)(2,1)S(1)}, bf16[32,1024,32]{1,2,0:T(8,128)(2,1)}, u32[]{:S(2)}, u32[]{:S(2)}) collective-permute-start(bf16[32,1024,32]{1,2,0:T(8,128)(2,1)S(1)} %collective-permute-done.2), channel_id=1, source_target_pairs={{0,2},{2,4},{4,6},{6,8},{8,10},{10,12},{12,14},{14,16},{16,18},{18... | collective-permute-start | bytes 6291464 | tf_op jit(solution)/shard_map/ppermute | solution.py:25
  381.3 94.6 %collective-permute-start.5 = (bf16[32,1024,32]{1,2,0:T(8,128)(2,1)}, bf16[32,1024,32]{1,2,0:T(8,128)(2,1)}, u32[]{:S(2)}, u32[]{:S(2)}) collective-permute-start(bf16[32,1024,32]{1,2,0:T(8,128)(2,1)} %collective-permute-done.3), channel_id=1, source_target_pairs={{0,30},{2,0},{4,2},{6,4},{8,6},{10,8},{12,10},{14,12},{16,14},{18,... | collective-permute-start | bytes 6291464 | tf_op jit(solution)/shard_map/ppermute | solution.py:30
  385.2 93.3 %collective-permute-start.6 = (bf16[32,1024,32]{1,2,0:T(8,128)(2,1)}, bf16[32,1024,32]{1,2,0:T(8,128)(2,1)}, u32[]{:S(2)}, u32[]{:S(2)}) collective-permute-start(bf16[32,1024,32]{1,2,0:T(8,128)(2,1)} %collective-permute-done.4), channel_id=1, source_target_pairs={{0,2},{2,4},{4,6},{6,8},{8,10},{10,12},{12,14},{14,16},{16,18},{18... | collective-permute-start | bytes 6291464 | tf_op jit(solution)/shard_map/ppermute | solution.py:25
  475.8 1980.0 %all-gather.24.cloned.1.call-start = ((), (), s32[]{:S(2)}) async-start(), calls=%async_computation.27 | async-start | bytes 2457600 | tf_op jit(solution)/shard_map/all_gather | solution.py:201
  475.9 175.4 %collective-permute-start.7 = (bf16[32,1024,32]{1,2,0:T(8,128)(2,1)}, bf16[32,1024,32]{1,2,0:T(8,128)(2,1)S(1)}, u32[]{:S(2)}, u32[]{:S(2)}) collective-permute-start(bf16[32,1024,32]{1,2,0:T(8,128)(2,1)} %collective-permute-done.5), channel_id=1, source_target_pairs={{0,30},{2,0},{4,2},{6,4},{8,6},{10,8},{12,10},{14,12},{16,14},{18,... | collective-permute-start | bytes 6291464 | tf_op jit(solution)/shard_map/ppermute | solution.py:30
  478.5 172.8 %collective-permute-start.8 = (bf16[32,1024,32]{1,2,0:T(8,128)(2,1)}, bf16[32,1024,32]{1,2,0:T(8,128)(2,1)}, u32[]{:S(2)}, u32[]{:S(2)}) collective-permute-start(bf16[32,1024,32]{1,2,0:T(8,128)(2,1)} %collective-permute-done.6), channel_id=1, source_target_pairs={{0,2},{2,4},{4,6},{6,8},{8,10},{10,12},{12,14},{14,16},{16,18},{18... | collective-permute-start | bytes 6291464 | tf_op jit(solution)/shard_map/ppermute | solution.py:25
  546.0 2144.5 %reduce-scatter.43.cloned.1.call-start = ((), (), s32[]{:S(2)}) async-start(), calls=%async_computation.35 | async-start | bytes 614400
  569.8 97.2 %copy-start.110 = (f32[16,32]{1,0:T(8,128)S(1)}, f32[16,32]{1,0:T(8,128)}, u32[]{:S(2)}) copy-start(f32[16,32]{1,0:T(8,128)} %param.24) | copy-start | bytes 6148
  650.7 795.1 %copy-start.111 = (s32[1600]{0:T(1024)}, s32[1600]{0:T(1024)S(1)}, u32[]{:S(2)}) copy-start(s32[1600]{0:T(1024)S(1)} %get-tuple-element.92) | copy-start | bytes 19204
  650.7 795.1 %copy-start.113 = (s32[1600]{0:T(1024)}, s32[1600]{0:T(1024)S(1)}, u32[]{:S(2)}) copy-start(s32[1600]{0:T(1024)S(1)} %get-tuple-element.93) | copy-start | bytes 19204
  651.3 700.7 %collective-permute-start.9 = (bf16[32,1024,32]{1,2,0:T(8,128)(2,1)S(1)}, bf16[32,1024,32]{1,2,0:T(8,128)(2,1)}, u32[]{:S(2)}, u32[]{:S(2)}) collective-permute-start(bf16[32,1024,32]{1,2,0:T(8,128)(2,1)S(1)} %collective-permute-done.7), channel_id=1, source_target_pairs={{0,30},{2,0},{4,2},{6,4},{8,6},{10,8},{12,10},{14,12},{16,14},{18,... | collective-permute-start | bytes 6291464 | tf_op jit(solution)/shard_map/ppermute | solution.py:30
  651.3 700.7 %collective-permute-start.10 = (bf16[32,1024,32]{1,2,0:T(8,128)(2,1)}, bf16[32,1024,32]{1,2,0:T(8,128)(2,1)}, u32[]{:S(2)}, u32[]{:S(2)}) collective-permute-start(bf16[32,1024,32]{1,2,0:T(8,128)(2,1)} %collective-permute-done.8), channel_id=1, source_target_pairs={{0,2},{2,4},{4,6},{6,8},{8,10},{10,12},{12,14},{14,16},{16,18},{18... | collective-permute-start | bytes 6291464 | tf_op jit(solution)/shard_map/ppermute | solution.py:25
  752.7 596.3 %copy-start.16 = (f32[512,32]{1,0:T(8,128)}, f32[512,32]{1,0:T(8,128)S(1)}, u32[]{:S(2)}) copy-start(f32[512,32]{1,0:T(8,128)S(1)} %all_gather.65) | copy-start | bytes 196612
  1352.0 23.9 collective-permute-start.11
  1352.0 28.8 collective-permute-start.12
  1375.9 748.0 %collective-permute-start.13 = (bf16[32,1024,32]{1,2,0:T(8,128)(2,1)}, bf16[32,1024,32]{1,2,0:T(8,128)(2,1)}, u32[]{:S(2)}, u32[]{:S(2)}) collective-permute-start(bf16[32,1024,32]{1,2,0:T(8,128)(2,1)} %collective-permute-done.11), channel_id=1, source_target_pairs={{0,30},{2,0},{4,2},{6,4},{8,6},{10,8},{12,10},{14,12},{16,14},{18,... | collective-permute-start | bytes 6291464 | tf_op jit(solution)/shard_map/ppermute | solution.py:30
  1380.8 842.5 %collective-permute-start.14 = (bf16[32,1024,32]{1,2,0:T(8,128)(2,1)}, bf16[32,1024,32]{1,2,0:T(8,128)(2,1)}, u32[]{:S(2)}, u32[]{:S(2)}) collective-permute-start(bf16[32,1024,32]{1,2,0:T(8,128)(2,1)} %collective-permute-done.12), channel_id=1, source_target_pairs={{0,2},{2,4},{4,6},{6,8},{8,10},{10,12},{12,14},{14,16},{16,18},{18... | collective-permute-start | bytes 6291464 | tf_op jit(solution)/shard_map/ppermute | solution.py:25
  2455.3 238.0 %reduce-scatter.45.cloned.1.call-start = ((), (), s32[]{:S(2)}) async-start(), calls=%async_computation.36 | async-start | bytes 614400
  2565.7 134.7 %reduce-scatter.27.cloned.1.call-start = ((), (), s32[]{:S(2)}) async-start(), calls=%async_computation.24 | async-start | bytes 2457600 | tf_op jit(solution)/shard_map/reduce_scatter | solution.py:231
  2569.5 134.9 %reduce-scatter.31.cloned.1.call-start = ((), (), s32[]{:S(2)}) async-start(), calls=%async_computation.28 | async-start | bytes 2457600 | tf_op jit(solution)/shard_map/reduce_scatter | solution.py:231
  2620.9 89.5 %reduce-scatter.25.cloned.1.call-start = ((), (), s32[]{:S(2)}) async-start(), calls=%async_computation.22 | async-start | bytes 2457600 | tf_op jit(solution)/shard_map/reduce_scatter | solution.py:188
  2651.0 69.0 %reduce-scatter.21.cloned.1.call-start = ((), (), s32[]{:S(2)}) async-start(), calls=%async_computation.18 | async-start | bytes 2457600 | tf_op jit(solution)/shard_map/reduce_scatter | solution.py:188
  2681.7 75.7 %all-gather.22.cloned.1.call-start = ((), (), s32[]{:S(2)}) async-start(), calls=%async_computation.25 | async-start | bytes 2457600 | tf_op jit(solution)/shard_map/all_gather | solution.py:255
  2727.6 59.7 %all-gather.26.cloned.1.call-start = ((), (), s32[]{:S(2)}) async-start(), calls=%async_computation.29 | async-start | bytes 2457600 | tf_op jit(solution)/shard_map/all_gather | solution.py:255
  2728.2 269.7 %all-reduce.17.cloned.1.call-start = ((), (), s32[]{:S(2)}) async-start(), calls=%async_computation.37 | async-start | bytes 2097152
  2841.2 158.3 %reduce-scatter.35.cloned.1.call-start = ((), (), s32[]{:S(2)}) async-start(), calls=%async_computation.31 | async-start | bytes 278528 | tf_op jit(solution)/shard_map/reduce_scatter | solution.py:312
  2845.1 176.4 %reduce-scatter.29.cloned.1.call-start = ((), (), s32[]{:S(2)}) async-start(), calls=%async_computation.26 | async-start | bytes 2457600 | tf_op jit(solution)/shard_map/reduce_scatter | solution.py:291
  2849.6 201.6 %reduce-scatter.33.cloned.1.call-start = ((), (), s32[]{:S(2)}) async-start(), calls=%async_computation.30 | async-start | bytes 2457600 | tf_op jit(solution)/shard_map/reduce_scatter | solution.py:291
  2880.3 505.8 %reduce-scatter.39.cloned.1.call-start = ((), (), s32[]{:S(2)}) async-start(), calls=%async_computation.33 | async-start | bytes 35651584 | tf_op jit(solution)/shard_map/reduce_scatter | solution.py:315
  2918.3 801.7 %reduce-scatter.41.cloned.1.call-start = ((), (), s32[]{:S(2)}) async-start(), calls=%async_computation.34 | async-start | bytes 35651584 | tf_op jit(solution)/shard_map/reduce_scatter | solution.py:318
  2988.8 868.6 %reduce-scatter.37.cloned.1.call-start = ((), (), s32[]{:S(2)}) async-start(), calls=%async_computation.32 | async-start | bytes 270336 | tf_op jit(solution)/shard_map/reduce_scatter | solution.py:327
  (116 other events, 1353.7 us)
Sparse Core Ops, SparseCore 0:
  56.1 27.7 all-gather.9
  86.0 27.9 all-gather.15
  146.3 24.3 reduce-scatter.18
  190.4 24.4 reduce-scatter.22
  220.7 27.9 all-gather.11
  250.1 27.9 all-gather.17
  279.6 307.6 all-gather.13
  589.5 28.0 all-gather.19
  619.1 27.9 all-gather.23
  2455.4 26.0 reduce-scatter.42
  2565.9 25.9 reduce-scatter.44
  2594.6 26.8 reduce-scatter.26
  2623.8 36.3 reduce-scatter.30
  2662.2 27.5 reduce-scatter.24
  2691.9 28.1 reduce-scatter.20
  2727.7 29.6 all-gather.21
  2759.4 27.9 all-gather.25
  2841.3 93.7 all-reduce.16
  2938.6 54.7 reduce-scatter.34
  2995.5 25.9 reduce-scatter.28
  3024.3 26.8 reduce-scatter.32
  3055.4 330.5 reduce-scatter.38
  3390.3 329.6 reduce-scatter.40
  3722.7 134.7 reduce-scatter.36
